TPU v7x, 512 devices: a 4x2x32 block of a 4x8x32 slice. The times are simulated.
512 devices in a mesh: grp: 2 (over y), seq: 32 (over z), head: 4 (over x), rep: 2 (over core).
Axes of the slice: x: 4, y: 2, z: 32, core: 2. Of those that a mesh axis runs over, the one named last changes fastest.
The devices are a block of a 4x8x32 slice.
Arguments:
- x_proj: bfloat16 [4, 32, 32, 4, 8192], P(('grp', 'rep'), None, 'seq', None, 'head'), parts along dimension 0, may hold values from -6 to 6
- gate_proj: bfloat16 [4, 32, 32, 4, 8192], P(('grp', 'rep'), None, 'seq', None, 'head'), parts along dimension 0, may hold values from -6 to 6
- bc_proj: bfloat16 [4, 32, 32, 4, 256], P(('grp', 'rep'), None, 'seq'), parts along dimension 0, may hold values from -6 to 6
- dt_proj: bfloat16 [4, 32, 32, 4, 128], P(('grp', 'rep'), None, 'seq', None, 'head'), parts along dimension 0, may hold values from -5.5 to 7.5
- a_rate: float32 [128], P('head'), may hold values from 2.4414063e-05 to 0.05
- dt_bias: float32 [128], P('head'), may hold values from -1 to 1
- d_skip: float32 [128], P('head'), may hold values from 0.5 to 1.5
- conv_x_weight: float32 [4, 8192], P(None, 'head'), may hold values from -3 to 3
- conv_bc_weight: float32 [4, 256], replicated, may hold values from -3 to 3
- norm_gain: float32 [8192], P('head'), may hold values from 0.1 to 1.9
- out_weight: bfloat16 [8192, 2048], P(('seq', 'rep'), 'head'), may hold values from -0.0625 to 0.0625
- request_first_position: int32 [4], P(('grp', 'rep')), parts along dimension 0, may hold values from 0 to 2047
- owner: int32 [4, 32], P(('grp', 'rep')), parts along dimension 0, may hold values from 0 to 31, each once within a row
Outputs:
- mixed: bfloat16 [4, 4096, 2048], P(('grp', 'rep'), 'seq', 'head'), parts along dimension 0
- ssm_state: float32 [4, 32, 128, 256], P(('grp', 'rep'), 'seq', 'head'), parts along dimension 0
- conv_x_state: bfloat16 [4, 32, 3, 256], P(('grp', 'rep'), 'seq', None, 'head'), parts along dimension 0
- conv_bc_state: bfloat16 [4, 32, 3, 8], P(('grp', 'rep'), 'seq'), parts along dimension 0
There are 2 independent parts, one for each index of `grp`. A program takes and returns all parts, laid end to end along the dimension named above; an argument that names none is the same for every part. Nothing has to cross between parts.
Inputs may be any that keep to these rules, and one draw needn't show every extreme that they name: Each row of owner names every index of seq once.
All inputs are finite; a program needn't handle non-finite values.
Results may differ from a plain program's by a relative error of at most 0.007.
Values may be sent and summed in bfloat16 or wider, within the bound.
A program may use at most 128 MiB of HBM per device.

v0:
```python
import jax
import jax.numpy as jnp
from jax import lax
from jax.sharding import PartitionSpec as P

HEAD_DIM = 64
NSTATE = 128
KCONV = 4
SPAN = 128
INNER = 8192
highest = lax.Precision.HIGHEST
stability_constant = 1e-05


def side_by_side(arrays, axis, split_dim, concat_dim, along):
    ends, at = ([], 0)
    for a in arrays[:-1]:
        at += a.shape[along]
        ends.append(at)
    both = jnp.concatenate(arrays, axis=along)
    return tuple(
        jnp.split(
            lax.all_to_all(both, axis, split_axis=split_dim, concat_axis=concat_dim, tiled=True),
            ends,
            axis=along,
        )
    )


def passed_along(value, axis, by):
    devices = lax.axis_size(axis)
    pairs = [(i, i + by) for i in range(devices) if 0 <= i + by < devices]
    return lax.ppermute(value, axis, pairs)


def prefix(value, axis, combine, identity):
    devices, place = (lax.axis_size(axis), lax.axis_index(axis))
    everything = jax.tree.map(lambda part: lax.all_gather(part, axis), value)
    start = jax.tree.map(
        lambda part, zero: jnp.broadcast_to(jnp.asarray(zero, part.dtype), part.shape),
        value,
        identity,
    )

    def lap(k, before):
        reached = k < place
        new = combine(before, jax.tree.map(lambda part: part[k], everything))
        return jax.tree.map(lambda a, b: jnp.where(reached, a, b), new, before)

    return lax.fori_loop(0, devices, lap, start)


def broadcast(block, axis, source):
    block = jnp.where(lax.axis_index(axis) == source, block, jnp.zeros_like(block))
    return lax.psum(block, axis)


def span_terms(x_conv, b_rows, c_rows, step_size, log_decay):
    cum_decay = jnp.cumsum(log_decay, axis=1)
    scores = jnp.einsum("kqn,ktn->kqt", c_rows, b_rows, preferred_element_type=jnp.float32)
    cum_heads = jnp.swapaxes(cum_decay, 1, 2)
    step_heads = jnp.swapaxes(step_size, 1, 2)
    block_len = cum_decay.shape[1]
    causal = jnp.arange(block_len)[:, None] >= jnp.arange(block_len)[None, :]
    decay_gap = cum_heads[:, :, :, None] - cum_heads[:, :, None, :]
    seg_decay = jnp.exp(jnp.where(causal, decay_gap, -jnp.inf))
    weights = (scores[:, None] * seg_decay * step_heads[:, :, None, :]).astype(jnp.bfloat16)
    y_intra = jnp.einsum("khqt,kthp->kqhp", weights, x_conv, preferred_element_type=jnp.float32)
    remaining_length = jnp.exp(cum_decay[:, -1:, :] - cum_decay)
    scaled = ((remaining_length * step_size)[..., None] * x_conv.astype(jnp.float32)).astype(
        jnp.bfloat16
    )
    states = jnp.einsum("kthp,ktn->khpn", scaled, b_rows, preferred_element_type=jnp.float32)
    return (cum_decay, y_intra, states, jnp.exp(cum_decay[:, -1, :]))


def conv_silu(preceding_tokens, current, weight):
    extended = jnp.concatenate([preceding_tokens, current], axis=0)
    length = current.shape[0]
    accum = jnp.zeros(current.shape, jnp.float32)
    for offset in range(weight.shape[0]):
        accum = accum + weight[offset] * extended[offset : offset + length].astype(jnp.float32)
    return jax.nn.silu(accum)


def link(preceding_tokens, later):
    return (
        preceding_tokens[0] * later[0],
        later[0][:, None, None] * preceding_tokens[1] + later[1],
    )


def add_rows(source, piece):
    return jnp.dot(source, piece, preferred_element_type=jnp.float32)


def take_slab(values, slab_index, seq_count):
    grouped = values.reshape(values.shape[0], seq_count, -1)
    return lax.dynamic_index_in_dim(grouped, slab_index, axis=1, keepdims=False)


def local(
    x_proj,
    gate_proj,
    bc_proj,
    dt_proj,
    a_rate,
    dt_bias,
    d_skip,
    conv_x_weight,
    conv_bc_weight,
    norm_gain,
    out_weight,
    request_first_position,
    owner,
):
    x_all, z_all, bc_all, dt_all = side_by_side(
        (x_proj, gate_proj, bc_proj, dt_proj), "seq", 1, 2, 4
    )
    tokens_here = x_all.shape[2] * x_all.shape[3]
    x_local = x_all.reshape(tokens_here, x_all.shape[4])
    z_local = z_all.reshape(tokens_here, z_all.shape[4])
    bc_local = bc_all.reshape(tokens_here, bc_all.shape[4])
    dt_local = dt_all.reshape(tokens_here, dt_all.shape[4])
    heads = dt_local.shape[1]
    seq_index = lax.axis_index("seq")
    seq_count = lax.axis_size("seq")
    positions = seq_index * tokens_here + jnp.arange(tokens_here, dtype=jnp.int32)
    is_live = positions >= request_first_position[0]
    x_live = jnp.where(is_live[:, None], x_local, jnp.zeros_like(x_local))
    bc_live = jnp.where(is_live[:, None], bc_local, jnp.zeros_like(bc_local))
    rim_rows = KCONV - 1
    tail_x = x_live[tokens_here - rim_rows :]
    tail_bc = bc_live[tokens_here - rim_rows :]
    before_x, before_bc = passed_along((tail_x, tail_bc), "seq", 1)
    x_conv = conv_silu(before_x, x_live, conv_x_weight).astype(jnp.bfloat16)
    bc_conv = conv_silu(before_bc, bc_live, conv_bc_weight).astype(jnp.bfloat16)
    step_size = (
        jax.nn.softplus(dt_local.astype(jnp.float32) + dt_bias)
        * is_live.astype(jnp.float32)[:, None]
    )
    log_decay = -a_rate * step_size
    blocks = tokens_here // SPAN
    x_blocks = x_conv.reshape(blocks, SPAN, heads, HEAD_DIM)
    b_blocks = bc_conv[:, :NSTATE].reshape(blocks, SPAN, NSTATE)
    c_blocks = bc_conv[:, NSTATE:].reshape(blocks, SPAN, NSTATE)
    cum_decay, y_intra, states, decays = span_terms(
        x_blocks,
        b_blocks,
        c_blocks,
        step_size.reshape(blocks, SPAN, heads),
        log_decay.reshape(blocks, SPAN, heads),
    )

    def advance(carry, inputs):
        factor, contrib = inputs
        return (factor[:, None, None] * carry + contrib, carry)

    zero_state = jnp.zeros((heads, HEAD_DIM, NSTATE), jnp.float32)
    local_final, local_enter = lax.scan(advance, zero_state, (decays, states))
    dev_decay = jnp.prod(decays, axis=0)
    ones_heads = jnp.ones((heads,), jnp.float32)
    enter_decay, enter_state = prefix(
        (dev_decay, local_final), "seq", link, (ones_heads, zero_state)
    )
    c_wide = c_blocks.astype(jnp.float32)
    before_block = jnp.concatenate([ones_heads[None], jnp.cumprod(decays, axis=0)[:-1]], axis=0)
    entering = local_enter + before_block[:, :, None, None] * enter_state[None]
    y_state = jnp.exp(cum_decay)[..., None] * jnp.einsum(
        "kqn,khpn->kqhp", c_wide, entering, precision=highest
    )
    y_total = y_intra + y_state + d_skip[:, None] * x_blocks.astype(jnp.float32)
    y_flat = y_total.reshape(tokens_here, heads * HEAD_DIM)
    gated = y_flat * jax.nn.silu(z_local.astype(jnp.float32))
    square_sums = lax.psum(jnp.sum(gated * gated, axis=1), "head")
    normed = (
        gated * lax.rsqrt(square_sums[:, None] / INNER + stability_constant) * norm_gain
    ).astype(jnp.bfloat16)
    last_index = seq_count - 1
    own_final = dev_decay[:, None, None] * enter_state + local_final
    final_state, keep_x, keep_bc = (
        broadcast(own_final, "seq", last_index),
        broadcast(tail_x.astype(jnp.float32), "seq", last_index).astype(tail_x.dtype),
        broadcast(tail_bc.astype(jnp.float32), "seq", last_index).astype(tail_bc.dtype),
    )
    slab_index = jnp.sum(
        jnp.where(owner[0] == seq_index, jnp.arange(seq_count, dtype=jnp.int32), 0)
    )
    ssm_state = take_slab(final_state.reshape(heads, -1), slab_index, seq_count)[None, None]
    conv_x_state = take_slab(keep_x, slab_index, seq_count)[None, None]
    conv_bc_state = take_slab(keep_bc, slab_index, seq_count)[None, None]
    features = lax.all_gather(normed, "head", axis=1, tiled=True)
    out_cols = out_weight.shape[1]
    mixed_sum = add_rows(features, lax.all_gather(out_weight, ("seq", "rep"), axis=0, tiled=True))
    mixed = mixed_sum.astype(jnp.bfloat16).reshape(1, tokens_here, out_cols)
    return (mixed, ssm_state, conv_x_state, conv_bc_state)


def solution(mesh):
    return jax.shard_map(
        local,
        mesh=mesh,
        in_specs=(
            P(("grp", "rep"), None, "seq", None, "head"),
            P(("grp", "rep"), None, "seq", None, "head"),
            P(("grp", "rep"), None, "seq", None, None),
            P(("grp", "rep"), None, "seq", None, "head"),
            P("head"),
            P("head"),
            P("head"),
            P(None, "head"),
            P(),
            P("head"),
            P(("seq", "rep"), "head"),
            P(("grp", "rep")),
            P(("grp", "rep"), None),
        ),
        out_specs=(
            P(("grp", "rep"), "seq", "head"),
            P(("grp", "rep"), "seq", "head", None),
            P(("grp", "rep"), "seq", None, "head"),
            P(("grp", "rep"), "seq", None, None),
        ),
        check_vma=False,
    )
```

profile of v0, /device:TPU:34, one launch (start us, length us, event | category | flops | bytes accessed | tf_op | source)
XLA Modules:
  0.0 893.1 jit_solution(16891518025906551019)
XLA Ops:
  8.1 2.9 pad_maximum_fusion
  10.9 45.8 %all-to-all-start = ((bf16[1,32,1,4,4384]{4,3,2,0,1:T(4,128)(2,1)}), bf16[1,32,1,4,4384]{4,3,2,0,1:T(4,128)(2,1)S(1)}, u32[]{:S(2)}, u32[]{:S(2)}) async-start(bf16[1,32,1,4,4384]{4,3,2,0,1:T(4,128)(2,1)} %pad_maximum_fusion), calls=%async_computation | async-start | bytes 2293760 | tf_op jit(solution)/shard_map/all_to_all | solution.py:23
  57.5 111.5 %all-to-all-done = bf16[1,32,1,4,4384]{4,3,2,0,1:T(4,128)(2,1)S(1)} async-done(((bf16[1,32,1,4,4384]{4,3,2,0,1:T(4,128)(2,1)}), bf16[1,32,1,4,4384]{4,3,2,0,1:T(4,128)(2,1)S(1)}, u32[]{:S(2)}, u32[]{:S(2)}) %all-to-all-start) | async-done | bytes 1122336 | tf_op jit(solution)/shard_map/all_to_all | solution.py:23
  169.4 0.3 slice_convert_fusion
  170.6 3.9 collective-permute-start
  174.6 1.9 collective-permute-start.1
  176.7 8.4 collective-permute-done.1
  185.2 2.9 fusion.8
  188.2 1.3 convolution_add_fusion
  189.6 58.3 %all-gather = f32[32,1,32]{2,1,0:T(1,128)S(1)} all-gather(f32[1,1,32]{2,1,0:T(1,128)S(1)} %get-tuple-element.155), channel_id=2, replica_groups=mesh['grp'=2,'seq'=32,'head'=4,'rep'=2] {'seq'}, dimensions={0}, use_global_device_ids=true | all-gather | bytes 4224 | tf_op jit(solution)/shard_map/all_gather | solution.py:38
  247.8 311.1 %all-gather.10.cloned.1.call-done = f32[1024,64,128]{2,1,0:T(8,128)} async-done(((f32[32,64,128]{2,1,0:T(8,128)}), f32[1024,64,128]{2,1,0:T(8,128)}) %all-gather.10.cloned.1.call-update) | async-done | bytes 33554448 | tf_op jit(solution)/shard_map/all_gather | solution.py:38
  559.0 48.1 %while.9 = (s32[]{:T(128)}, f32[32,64,128]{2,1,0:T(8,128)S(1)}, s32[]{:T(128)}, f32[32,32]{1,0:T(8,128)S(1)}, f32[32,32,64,128]{3,2,1,0:T(8,128)}, /*index=5*/s32[]{:T(128)}, s32[]{:T(128)}) while((s32[]{:T(128)}, f32[32,64,128]{2,1,0:T(8,128)S(1)}, s32[]{:T(128)}, f32[32,32]{1,0:T(8,128)S(1)}, f32[32,32,64,128]{3,2,1,0:T(8,128)}, ...), condition=%wide.region_2.3_spmd.clone, body=%wide.region_1.2_spmd.clone.sunk | while | flops 1048580 | bytes 3146217 | solution.py:50
  559.0 1.5 fusion.43
  560.5 1.5 fusion.43
  562.0 1.5 fusion.43
  563.6 1.5 fusion.43
  565.1 1.5 fusion.43
  566.6 1.5 fusion.43
  568.1 1.5 fusion.43
  569.6 1.5 fusion.43
  571.1 1.5 fusion.43
  572.6 1.5 fusion.43
  574.1 1.5 fusion.43
  575.6 1.5 fusion.43
  577.1 1.5 fusion.43
  578.6 1.5 fusion.43
  580.1 1.5 fusion.43
  581.6 1.5 fusion.43
  583.1 1.5 fusion.43
  584.6 1.5 fusion.43
  586.1 1.5 fusion.43
  587.6 1.5 fusion.43
  589.1 1.5 fusion.43
  590.6 1.5 fusion.43
  592.1 1.5 fusion.43
  593.6 1.5 fusion.43
  595.1 1.5 fusion.43
  596.6 1.5 fusion.43
  598.1 1.5 fusion.43
  599.6 1.5 fusion.43
  601.1 1.5 fusion.43
  602.6 1.5 fusion.43
  604.1 1.5 fusion.43
  605.6 1.5 fusion.43
  607.1 1.2 add_select_fusion
  608.3 2.5 reshape_reshape.3
  610.9 0.6 all-gather.8.cloned.1.call-update
  611.6 2.4 reshape.434
  614.0 1.4 reshape.433
  615.5 3.8 copy.93
  619.3 0.3 copy.91
  619.8 0.6 fusion.1
  620.4 0.4 copy-done.4
  621.0 1.1 multiply_reduce_fusion
  622.1 8.8 psum.28
  630.9 1.2 fusion.7
  632.2 0.6 fusion.31
  635.0 137.0 %all-reduce = (bf16[3,2048]{0,1:T(8,128)(2,1)S(1)}, bf16[3,256]{1,0:T(4,128)(2,1)S(1)}) all-reduce(f32[3,2048]{0,1:T(8,128)S(1)} %convert_select_fusion, f32[3,256]{1,0:T(4,128)S(1)} %convert_select_fusion.1), channel_id=1, replica_groups=mesh['grp'=2,'seq'=32,'head'=4,'rep'=2] {'seq'}, use_global_device_ids=true, to_apply=%region_7.8 | all-reduce | flops 6912 | bytes 41472 | tf_op jit(solution)/shard_map/psum | solution.py:55
  772.1 0.6 copy.101
  772.6 0.7 copy.97
  773.3 104.8 %all-reduce.3.cloned.1.call-done = f32[32,32,256]{2,1,0:T(8,128)} async-done(((f32[32,32,256]{2,1,0:T(8,128)}), f32[32,32,256]{2,1,0:T(8,128)}) %all-reduce.3.cloned.1.call-update) | async-done | bytes 1048592 | tf_op jit(solution)/shard_map/psum | solution.py:55
  878.1 1.0 constant_dynamic-slice_fusion.2
  879.0 0.6 copy.100
  879.7 6.0 fusion.4
  (99 shorter events, 2.9 us)
Async XLA Ops:
  8.0 49.4 %copy-start.10 = (f32[32]{0:T(128)S(1)}, f32[32]{0:T(128)}, u32[]{:S(2)}) copy-start(f32[32]{0:T(128)} %param.19) | copy-start | bytes 388
  8.0 49.4 %copy-start.8 = (f32[4,256]{1,0:T(4,128)S(1)}, f32[4,256]{1,0:T(4,128)}, u32[]{:S(2)}) copy-start(f32[4,256]{1,0:T(4,128)} %param.23) | copy-start | bytes 12292
  8.1 49.4 %copy-start.6 = (f32[4,2048]{1,0:T(4,128)S(1)}, f32[4,2048]{1,0:T(4,128)}, u32[]{:S(2)}) copy-start(f32[4,2048]{1,0:T(4,128)} %param.22) | copy-start | bytes 98308
  8.1 161.0 %copy-start.9 = (f32[32]{0:T(128)S(1)}, f32[32]{0:T(128)}, u32[]{:S(2)}) copy-start(f32[32]{0:T(128)} %param.20) | copy-start | bytes 388
  10.9 158.1 %all-to-all-start = ((bf16[1,32,1,4,4384]{4,3,2,0,1:T(4,128)(2,1)}), bf16[1,32,1,4,4384]{4,3,2,0,1:T(4,128)(2,1)S(1)}, u32[]{:S(2)}, u32[]{:S(2)}) async-start(bf16[1,32,1,4,4384]{4,3,2,0,1:T(4,128)(2,1)} %pad_maximum_fusion), calls=%async_computation | async-start | bytes 2293760 | tf_op jit(solution)/shard_map/all_to_all | solution.py:23
  56.7 502.2 %all-gather.10.cloned.1.call-start = ((), (), s32[]{:S(2)}) async-start(), calls=%async_computation.4 | async-start | bytes 34603008 | tf_op jit(solution)/shard_map/all_gather | solution.py:38
  170.3 19.1 %copy-start.1 = (bf16[128,2048]{0,1:T(8,128)(2,1)}, bf16[128,2048]{0,1:T(8,128)(2,1)S(1)}, u32[]{:S(2)}) copy-start(bf16[128,2048]{0,1:T(8,128)(2,1)S(1)} %broadcast_select_fusion) | copy-start | bytes 1572868
  170.6 14.6 %collective-permute-start = (bf16[3,2048]{0,1:T(8,128)(2,1)S(1)}, bf16[3,2048]{0,1:T(8,128)(2,1)S(1)}, u32[]{:S(2)}, u32[]{:S(2)}) collective-permute-start(bf16[3,2048]{0,1:T(8,128)(2,1)S(1)} %slice.77), channel_id=1, source_target_pairs={{0,8},{8,16},{16,24},{24,32},{32,40},{40,48},{48,56},{56,64},{64,7... | collective-permute-start | bytes 36872 | tf_op jit(solution)/shard_map/ppermute | solution.py:33
  174.6 10.5 %collective-permute-start.1 = (bf16[3,256]{1,0:T(4,128)(2,1)S(1)}, bf16[3,256]{1,0:T(4,128)(2,1)S(1)}, u32[]{:S(2)}, u32[]{:S(2)}) collective-permute-start(bf16[3,256]{1,0:T(4,128)(2,1)S(1)} %slice.82), channel_id=1, source_target_pairs={{0,8},{8,16},{16,24},{24,32},{32,40},{40,48},{48,56},{56,64},{64,7... | collective-permute-start | bytes 4616 | tf_op jit(solution)/shard_map/ppermute | solution.py:33
  189.5 688.6 %all-reduce.3.cloned.1.call-start = ((), (), s32[]{:S(2)}) async-start(), calls=%async_computation.3 | async-start | bytes 2097152 | tf_op jit(solution)/shard_map/psum | solution.py:55
  559.0 48.1 %copy-start = (f32[32,64,128]{2,1,0:T(8,128)S(1)}, f32[32,64,128]{2,1,0:T(8,128)}, u32[]{:S(2)}) copy-start(f32[32,64,128]{2,1,0:T(8,128)} %convolution_add_fusion) | copy-start | bytes 3145732
  610.8 268.8 %all-gather.8.cloned.1.call-start = ((), (), s32[]{:S(2)}) async-start(), calls=%async_computation.2 | async-start | bytes 8519680 | tf_op jit(solution)/shard_map/all_gather | solution.py:194
  611.5 268.2 %all-gather.6.cloned.1.call-start = ((), (), s32[]{:S(2)}) async-start(), calls=%async_computation.1 | async-start | bytes 2621440 | tf_op jit(solution)/shard_map/all_gather | solution.py:192
  615.3 3.9 copy-start.3
  619.3 1.1 copy-start.11
  619.6 1.2 copy-start.4
  619.6 1.4 copy-start.5
  621.0 9.9 %copy-start.7 = (f32[2048]{0:T(1024)S(1)}, f32[2048]{0:T(1024)}, u32[]{:S(2)}) copy-start(f32[2048]{0:T(1024)} %param.24) | copy-start | bytes 24580
  622.1 10.1 %copy-start.12 = (s32[1,32]{1,0:T(1,128)S(1)}, s32[1,32]{1,0:T(1,128)}, u32[]{:S(2)}) copy-start(s32[1,32]{1,0:T(1,128)} %param.27) | copy-start | bytes 388
  622.1 12.7 %copy-start.2 = (bf16[128,2048]{0,1:T(8,128)(2,1)S(1)}, bf16[128,2048]{0,1:T(8,128)(2,1)}, u32[]{:S(2)}) copy-start(bf16[128,2048]{0,1:T(8,128)(2,1)} %copy-done.1) | copy-start | bytes 1572868
Sparse Core Ops, SparseCore 0:
  189.6 369.2 all-gather.9
  611.0 267.0 all-reduce.2
Sparse Core Ops, SparseCore 1:
  613.5 145.7 all-gather.7
  761.3 36.1 all-gather.5
where the time goes:
time: 895 us; the launch traced here: 893 us
  waiting for transfers between devices  537 us (60%)
  blocking collectives  204 us (23%)
  other arithmetic  56.9 us (6%)
  starting transfers between devices  51.9 us (6%)
  between operations  18.5 us (2%)
  local copies, waits for them, and re-layouts  15.2 us (2%)
  matrix products  9.14 us (1%)
    all_gather x1, waiting for transfers between devices, prefix(): everything = jax.tree.map(lambda part: lax.all_gather(part, axis), value)  311 us
    psum x1, blocking collectives, broadcast(): return lax.psum(block, axis)  137 us
    all_to_all x1, waiting for transfers between devices, side_by_side(): lax.all_to_all(both, axis, split_axis=split_dim, concat_axis=concat_dim,...  112 us
    psum x1, waiting for transfers between devices, broadcast(): return lax.psum(block, axis)  105 us
    all_gather x1, blocking collectives, prefix(): everything = jax.tree.map(lambda part: lax.all_gather(part, axis), value)  58.3 us
    select_n x32, other arithmetic, lap(): return jax.tree.map(lambda a, b: jnp.where(reached, a, b), new, before)  46.9 us
    all_to_all x1, starting transfers between devices, side_by_side(): lax.all_to_all(both, axis, split_axis=split_dim, concat_axis=concat_dim,...  45.8 us
  transfers between devices with their start and end apart: 7, of which 4 were waited for; matrix products, arithmetic and copies ran while one was open for 2% of the time, Pallas kernels for 0%

commit v1 on v0

--- a/solution.py
+++ b/solution.py
@@ -52,7 +52,7 @@
 
 def broadcast(block, axis, source):
     block = jnp.where(lax.axis_index(axis) == source, block, jnp.zeros_like(block))
-    return lax.psum(block, axis)
+    return jnp.sum(lax.all_gather(block, axis_name=axis), axis=0)
 
 
 def span_terms(x_conv, b_rows, c_rows, step_size, log_decay):

time: 895 us -> 1140 us (1.27)
  the two profiles are of different devices: /device:TPU:34 before, /device:TPU:33 now
where the time goes in v1:
time: 1140 us
  waiting for transfers between devices  818 us (72%)
  blocking collectives  155 us (14%)
  other arithmetic  69.8 us (6%)
  starting transfers between devices  51.6 us (5%)
  between operations  16.8 us (1%)
  local copies, waits for them, and re-layouts  15.9 us (1%)
    all_gather x1, waiting for transfers between devices, broadcast(): return jnp.sum(lax.all_gather(block, axis_name=axis), axis=0)  377 us
    all_gather x1, waiting for transfers between devices, prefix(): everything = jax.tree.map(lambda part: lax.all_gather(part, axis), value)  315 us
    all_to_all x1, waiting for transfers between devices, side_by_side(): lax.all_to_all(both, axis, split_axis=split_dim, concat_axis=concat_dim,...  112 us
    all_gather x2, blocking collectives, broadcast(): return jnp.sum(lax.all_gather(block, axis_name=axis), axis=0)  97.9 us
    all_gather x1, blocking collectives, prefix(): everything = jax.tree.map(lambda part: lax.all_gather(part, axis), value)  48.6 us
    select_n x32, other arithmetic, lap(): return jax.tree.map(lambda a, b: jnp.where(reached, a, b), new, before)  46.9 us
    all_to_all x1, starting transfers between devices, side_by_side(): lax.all_to_all(both, axis, split_axis=split_dim, concat_axis=concat_dim,...  46.3 us
  transfers between devices with their start and end apart: 7, of which 5 were waited for; matrix products, arithmetic and copies ran while one was open for 7% of the time, Pallas kernels for 0%

profile of v1, /device:TPU:33, one launch (start us, length us, event | category | flops | bytes accessed | tf_op | source)
XLA Modules:
  0.0 1138.2 jit_solution(5737713382696392021)
XLA Ops:
  7.2 2.9 pad_maximum_fusion
  10.1 46.3 %all-to-all-start = ((bf16[1,32,1,4,4384]{4,3,2,0,1:T(4,128)(2,1)}), bf16[1,32,1,4,4384]{4,3,2,0,1:T(4,128)(2,1)S(1)}, u32[]{:S(2)}, u32[]{:S(2)}) async-start(bf16[1,32,1,4,4384]{4,3,2,0,1:T(4,128)(2,1)} %pad_maximum_fusion), calls=%async_computation | async-start | bytes 2293760 | tf_op jit(solution)/shard_map/all_to_all | solution.py:23
  57.2 111.7 %all-to-all-done = bf16[1,32,1,4,4384]{4,3,2,0,1:T(4,128)(2,1)S(1)} async-done(((bf16[1,32,1,4,4384]{4,3,2,0,1:T(4,128)(2,1)}), bf16[1,32,1,4,4384]{4,3,2,0,1:T(4,128)(2,1)S(1)}, u32[]{:S(2)}, u32[]{:S(2)}) %all-to-all-start) | async-done | bytes 1122336 | tf_op jit(solution)/shard_map/all_to_all | solution.py:23
  170.1 3.1 collective-permute-start.1
  173.3 1.3 copy.124
  174.7 2.0 collective-permute-start
  176.7 0.7 collective-permute-done
  177.5 2.0 multiply_convert_fusion.3
  179.7 1.2 convolution_add_fusion
  181.1 0.7 all-gather.14.cloned.1.call-update
  181.9 2.4 reshape.432
  184.3 1.3 reshape.431
  185.8 2.7 copy.129
  188.5 48.6 %all-gather = f32[32,1,32]{2,1,0:T(1,128)S(1)} all-gather(f32[1,1,32]{2,1,0:T(1,128)S(1)} %get-tuple-element.153), channel_id=2, replica_groups=mesh['grp'=2,'seq'=32,'head'=4,'rep'=2] {'seq'}, dimensions={0}, use_global_device_ids=true | all-gather | bytes 4224 | tf_op jit(solution)/shard_map/all_gather | solution.py:38
  237.2 1.2 copy.126
  238.6 314.9 %all-gather.16.cloned.1.call-done = f32[1024,64,128]{2,1,0:T(8,128)} async-done(((f32[32,64,128]{2,1,0:T(8,128)}), f32[1024,64,128]{2,1,0:T(8,128)}) %all-gather.16.cloned.1.call-update) | async-done | bytes 33554448 | tf_op jit(solution)/shard_map/all_gather | solution.py:38
  553.5 48.2 %while.9 = (s32[]{:T(128)}, f32[32,64,128]{2,1,0:T(8,128)S(1)}, s32[]{:T(128)}, f32[32,32]{1,0:T(8,128)S(1)}, f32[32,32,64,128]{3,2,1,0:T(8,128)}, /*index=5*/s32[]{:T(128)}, s32[]{:T(128)}) while((s32[]{:T(128)}, f32[32,64,128]{2,1,0:T(8,128)S(1)}, s32[]{:T(128)}, f32[32,32]{1,0:T(8,128)S(1)}, f32[32,32,64,128]{3,2,1,0:T(8,128)}, ...), condition=%wide.region_2.3_spmd.clone, body=%wide.region_1.2_spmd.clone.sunk | while | flops 1048580 | bytes 3146217 | solution.py:50
  553.5 1.5 fusion.39
  555.0 1.5 fusion.39
  556.5 1.5 fusion.39
  558.0 1.5 fusion.39
  559.5 1.5 fusion.39
  561.0 1.5 fusion.39
  562.5 1.5 fusion.39
  564.0 1.5 fusion.39
  565.5 1.5 fusion.39
  567.0 1.5 fusion.39
  568.5 1.5 fusion.39
  570.0 1.5 fusion.39
  571.5 1.5 fusion.39
  573.0 1.5 fusion.39
  574.5 1.5 fusion.39
  576.0 1.5 fusion.39
  577.5 1.5 fusion.39
  579.0 1.5 fusion.39
  580.5 1.5 fusion.39
  582.1 1.5 fusion.39
  583.6 1.5 fusion.39
  585.1 1.5 fusion.39
  586.6 1.5 fusion.39
  588.1 1.5 fusion.39
  589.6 1.5 fusion.39
  591.1 1.5 fusion.39
  592.6 1.5 fusion.39
  594.2 1.5 fusion.39
  595.7 1.5 fusion.39
  597.2 1.5 fusion.39
  598.7 1.5 fusion.39
  600.2 1.5 fusion.39
  602.3 0.6 copy-done.3
  602.9 2.0 multiply_reduce_fusion
  605.0 2.6 copy.127
  607.6 8.6 psum.7
  616.2 2.4 multiply_convert_fusion.2
  618.8 1.1 add_select_fusion
  620.0 0.6 fusion.27
  622.5 0.8 select_bitcast_fusion
  623.3 55.6 %all-gather.5 = f32[32,3,2048]{2,1,0:T(4,128)S(1)} all-gather(f32[1,3,2048]{2,1,0:T(4,128)S(1)} %select_bitcast_fusion), channel_id=5, replica_groups=mesh['grp'=2,'seq'=32,'head'=4,'rep'=2] {'seq'}, dimensions={0}, use_global_device_ids=true | all-gather | bytes 811008 | tf_op jit(solution)/shard_map/all_gather | solution.py:55
  679.8 42.4 %all-gather.6 = f32[32,3,256]{2,1,0:T(4,128)S(1)} all-gather(f32[1,3,256]{2,1,0:T(4,128)S(1)} %select_bitcast_fusion.1), channel_id=6, replica_groups=mesh['grp'=2,'seq'=32,'head'=4,'rep'=2] {'seq'}, dimensions={0}, use_global_device_ids=true | all-gather | bytes 101376 | tf_op jit(solution)/shard_map/all_gather | solution.py:55
  722.9 13.4 %all-gather.12.cloned.1.call-done = bf16[128,8192]{1,0:T(8,128)(2,1)} async-done(((bf16[128,2048]{1,0:T(8,128)(2,1)}), bf16[128,8192]{1,0:T(8,128)(2,1)}) %all-gather.12.cloned.1.call-update) | async-done | bytes 2097168 | tf_op jit(solution)/shard_map/all_gather | solution.py:192
  736.3 5.9 fusion.4
  742.2 376.6 %all-gather.18.cloned.1.call-done = f32[1024,64,128]{2,1,0:T(8,128)} async-done(((f32[32,64,128]{2,1,0:T(8,128)}), f32[1024,64,128]{2,1,0:T(8,128)}) %all-gather.18.cloned.1.call-update) | async-done | bytes 33554448 | tf_op jit(solution)/shard_map/all_gather | solution.py:55
  1118.8 11.8 %reduce_sum.46 = f32[32,64,128]{2,1,0:T(8,128)S(1)} reduce(f32[32,32,64,128]{3,2,1,0:T(8,128)} %bitcast.95, f32[]{:T(128)} %constant.79.clone.1), dimensions={0}, to_apply=%region_5.6 | reduce | flops 8126464 | bytes 34603012 | tf_op jit(solution)/shard_map/reduce_sum | solution.py:55
  1131.0 0.6 copy.139
  (104 shorter events, 5.5 us)
Async XLA Ops:
  7.2 49.9 %copy-start.8 = (f32[32]{0:T(128)S(1)}, f32[32]{0:T(128)}, u32[]{:S(2)}) copy-start(f32[32]{0:T(128)} %param.19) | copy-start | bytes 388
  7.2 50.0 %copy-start.6 = (f32[4,256]{1,0:T(4,128)S(1)}, f32[4,256]{1,0:T(4,128)}, u32[]{:S(2)}) copy-start(f32[4,256]{1,0:T(4,128)} %param.23) | copy-start | bytes 12292
  7.2 50.0 %copy-start.4 = (f32[4,2048]{1,0:T(4,128)S(1)}, f32[4,2048]{1,0:T(4,128)}, u32[]{:S(2)}) copy-start(f32[4,2048]{1,0:T(4,128)} %param.22) | copy-start | bytes 98308
  7.2 161.7 %copy-start.7 = (f32[32]{0:T(128)S(1)}, f32[32]{0:T(128)}, u32[]{:S(2)}) copy-start(f32[32]{0:T(128)} %param.20) | copy-start | bytes 388
  10.1 158.8 %all-to-all-start = ((bf16[1,32,1,4,4384]{4,3,2,0,1:T(4,128)(2,1)}), bf16[1,32,1,4,4384]{4,3,2,0,1:T(4,128)(2,1)S(1)}, u32[]{:S(2)}, u32[]{:S(2)}) async-start(bf16[1,32,1,4,4384]{4,3,2,0,1:T(4,128)(2,1)} %pad_maximum_fusion), calls=%async_computation | async-start | bytes 2293760 | tf_op jit(solution)/shard_map/all_to_all | solution.py:23
  56.4 497.1 %all-gather.16.cloned.1.call-start = ((), (), s32[]{:S(2)}) async-start(), calls=%async_computation.3 | async-start | bytes 34603008 | tf_op jit(solution)/shard_map/all_gather | solution.py:38
  170.0 9.5 copy-start.2
  170.1 6.6 collective-permute-start.1
  174.7 2.8 collective-permute-start
  181.0 541.8 %all-gather.14.cloned.1.call-start = ((), (), s32[]{:S(2)}) async-start(), calls=%async_computation.2 | async-start | bytes 8519680 | tf_op jit(solution)/shard_map/all_gather | solution.py:194
  181.8 554.4 %all-gather.12.cloned.1.call-start = ((), (), s32[]{:S(2)}) async-start(), calls=%async_computation.1 | async-start | bytes 2621440 | tf_op jit(solution)/shard_map/all_gather | solution.py:192
  601.7 1.2 copy-start.3
  601.7 1.2 copy-start.9
  605.0 11.2 copy-start.1
  605.0 11.2 copy-start.5
  607.6 11.1 copy-start
  618.7 500.1 %all-gather.18.cloned.1.call-start = ((), (), s32[]{:S(2)}) async-start(), calls=%async_computation.4 | async-start | bytes 34603008 | tf_op jit(solution)/shard_map/all_gather | solution.py:55
  618.8 1.2 copy-start.10
Sparse Core Ops, SparseCore 0:
  181.2 372.3 all-gather.15
  555.6 139.6 all-gather.13
  697.4 38.7 all-gather.11
  738.2 380.5 all-gather.17
